TPU v7x, 32 devices: a whole 2x2x4 slice. The times are simulated.
32 devices in a mesh: shard: 32 (over z, y, x, core).
Axes of the slice: x: 2, y: 2, z: 4, core: 2. Of those that a mesh axis runs over, the one named last changes fastest.
Arguments:
- picked_rows: int32 [1024, 8], P('shard'), may hold values from 0 to 16383
- main_table: float32 [16384, 128], P('shard'), may hold values from -6 to 6
- dense_part: float32 [1024, 128], P('shard'), may hold values from -6 to 6
- small_ids: int32 [1024], P('shard'), may hold values from 0 to 127
- small_table: float32 [128, 128], P('shard'), may hold values from -6 to 6
- scale_ids: int32 [1024], P('shard'), may hold values from 0 to 127
Outputs:
- features: float32 [1024, 3, 128], P('shard')
All inputs are finite; a program needn't handle non-finite values.
Results may differ from a plain program's by a relative error of at most 0.0003.
Values sent between devices are 32-bit elements.
A program may use at most 64 MiB of HBM per device.

v0:
```python
import jax
import jax.numpy as jnp
from jax import lax
from jax.sharding import PartitionSpec as P

PICKS = 8


def summed_rows(term, span, axis):
    whole = term(jnp.int32(0), span * lax.axis_size(axis))
    return lax.psum_scatter(whole, axis, scatter_dimension=0, tiled=True)


def rows_here(table_part, wanted, first_row):
    place = wanted - first_row
    inside = (place >= 0) & (place < table_part.shape[0])
    found = jnp.take(table_part, jnp.clip(place, 0, table_part.shape[0] - 1), axis=0).astype(
        jnp.float32
    )
    return jnp.where(inside[..., None], found, 0.0)


def local(picked_rows, main_table, dense_part, small_ids, small_table, scale_ids):
    big_first = lax.axis_index("shard") * main_table.shape[0]
    all_ids = lax.all_gather(picked_rows, "shard", axis=0, tiled=True)

    def pooled_part(start, count):
        wanted = lax.dynamic_slice_in_dim(all_ids, start, count)
        return jnp.sum(rows_here(main_table, wanted, big_first), axis=1)

    pooled = summed_rows(pooled_part, picked_rows.shape[0], "shard") * PICKS ** (-0.5)
    every_row = lax.all_gather(small_table, "shard", axis=0, tiled=True)
    small_rows = jnp.take(every_row, small_ids, axis=0).astype(jnp.float32)
    scale_rows = jnp.take(every_row, scale_ids, axis=0).astype(jnp.float32)
    dense_part = dense_part * scale_rows
    features = jnp.stack(
        [dense_part * pooled, pooled * small_rows, dense_part * small_rows], axis=1
    )
    return features


def solution(mesh):
    placed = (
        P("shard", None),
        P("shard", None),
        P("shard", None),
        P("shard"),
        P("shard", None),
        P("shard"),
    )
    return jax.shard_map(
        local, mesh=mesh, in_specs=placed, out_specs=P("shard", None, None), check_vma=False
    )
```

profile of v0, /device:TPU:0, one launch (start us, length us, event | category | flops | bytes accessed | tf_op | source)
XLA Modules:
  0.0 228.5 jit_solution(12690492039786159335)
XLA Ops:
  6.5 0.0 copy-start
  6.5 0.0 reduce-scatter.2.cloned.1.call-start
  6.5 44.0 %all-gather.1 = s32[32,32,8]{1,2,0:T(8,128)S(1)} all-gather(s32[1,32,8]{1,2,0:T(8,128)} %bitcast.21), channel_id=1, replica_groups=mesh['shard'=32] {'shard'}, dimensions={0}, use_global_device_ids=true | all-gather | bytes 33792 | tf_op jit(solution)/shard_map/all_gather | solution.py:25
  50.6 0.1 reshape.51
  50.7 0.2 copy.16
  50.9 0.3 reshape.29
  51.2 0.3 copy.15
  51.5 0.3 copy.17
  51.8 0.0 copy-done
  51.8 27.8 %gather_fusion = f32[8192,128]{1,0:T(8,128)} fusion(f32[512,128]{1,0:T(8,128)S(1)} %copy-done, s32[8192]{0:T(1024)S(1)} %broadcast_clamp_fusion), kind=kCustom, calls=%fused_computation.2 | custom fusion | bytes 8421376 | tf_op jit(solution)/shard_map/jit(_take)/gather | solution.py:17
  79.6 0.0 copy-start.2
  79.6 0.0 copy-start.3
  79.6 0.0 copy-start.4
  79.6 0.0 copy-start.1
  79.6 8.7 %fusion.1 = f32[1024,128]{1,0:T(8,128)} fusion(f32[8192,128]{1,0:T(8,128)} %gather_fusion, pred[1024,8]{1,0:T(8,128)(4,1)S(1)} %copy.15, pred[1024,8]{1,0:T(8,128)(4,1)S(1)} %bitcast.20), kind=kLoop, calls=%fused_computation.5 | loop fusion | flops 3014656 | bytes 4734976 | tf_op jit(solution)/shard_map/reduce_sum | solution.py:29
  88.3 0.0 reduce-scatter.2.cloned.1.call-update
  88.3 0.0 copy-done.2
  88.4 36.8 %all-gather = f32[32,4,128]{2,1,0:T(4,128)S(1)} all-gather(f32[1,4,128]{2,1,0:T(4,128)S(1)} %bitcast.22), channel_id=1, replica_groups=mesh['shard'=32] {'shard'}, dimensions={0}, use_global_device_ids=true | all-gather | bytes 67584 | tf_op jit(solution)/shard_map/all_gather | solution.py:32
  125.2 0.0 copy-done.3
  125.2 0.6 gather_fusion.1
  125.8 0.0 copy-done.4
  125.8 0.6 gather_fusion.2
  126.4 93.9 %reduce-scatter.2.cloned.1.call-done = f32[32,128]{1,0:T(8,128)} async-done(((f32[1024,128]{1,0:T(8,128)}), f32[32,128]{1,0:T(8,128)}) %reduce-scatter.2.cloned.1.call-update) | async-done | bytes 16400 | tf_op jit(solution)/shard_map/reduce_scatter | solution.py:11
  220.3 0.0 copy-done.1
  220.3 0.8 multiply_bitcast_fusion.2
  221.1 0.6 pad_maximum_fusion
  (11 shorter events, 0.1 us)
Async XLA Ops:
  6.5 45.2 %copy-start = (f32[512,128]{1,0:T(8,128)S(1)}, f32[512,128]{1,0:T(8,128)}, u32[]{:S(2)}) copy-start(f32[512,128]{1,0:T(8,128)} %param.9) | copy-start | bytes 786436
  6.5 213.7 %reduce-scatter.2.cloned.1.call-start = ((), (), s32[]{:S(2)}) async-start(), calls=%async_computation.1 | async-start | bytes 540672 | tf_op jit(solution)/shard_map/reduce_scatter | solution.py:11
  79.6 8.7 %copy-start.2 = (f32[4,128]{1,0:T(4,128)S(1)}, f32[4,128]{1,0:T(4,128)}, u32[]{:S(2)}) copy-start(f32[4,128]{1,0:T(4,128)} %param.12) | copy-start | bytes 6148
  79.6 45.6 %copy-start.3 = (s32[32]{0:T(128)S(1)}, s32[32]{0:T(128)}, u32[]{:S(2)}) copy-start(s32[32]{0:T(128)} %param.13) | copy-start | bytes 388
  79.6 46.1 %copy-start.4 = (s32[32]{0:T(128)S(1)}, s32[32]{0:T(128)}, u32[]{:S(2)}) copy-start(s32[32]{0:T(128)} %param.11) | copy-start | bytes 388
  79.6 140.6 %copy-start.1 = (f32[32,128]{1,0:T(8,128)S(1)}, f32[32,128]{1,0:T(8,128)}, u32[]{:S(2)}) copy-start(f32[32,128]{1,0:T(8,128)} %param.10) | copy-start | bytes 49156
Sparse Core Ops, SparseCore 0:
  88.5 131.7 reduce-scatter.1
where the time goes:
time: 229 us
  waiting for transfers between devices  93.9 us (41%)
  blocking collectives  80.8 us (35%)
  local copies, waits for them, and re-layouts  30.1 us (13%)
  between operations  13.5 us (6%)
  other arithmetic  10.2 us (4%)
    reduce_scatter x1, waiting for transfers between devices, summed_rows(): return lax.psum_scatter(whole, axis, scatter_dimension=0, tiled=True)  93.9 us
    all_gather x1, blocking collectives, local(): all_ids = lax.all_gather(picked_rows, 'shard', axis=0, tiled=True)  44 us
    all_gather x1, blocking collectives, local(): every_row = lax.all_gather(small_table, 'shard', axis=0, tiled=True)  36.8 us
    gather x1, local copies, waits for them, and re-layouts, rows_here(): jnp.take(table_part, jnp.clip(place, 0, table_part.shape[0] - 1), axis=0)  27.8 us
    reduce_sum x1, other arithmetic, pooled_part(): return jnp.sum(rows_here(main_table, wanted, big_first), axis=1)  8.69 us
  transfers between devices with their start and end apart: 1, of which 1 were waited for; matrix products, arithmetic and copies ran while one was open for 1% of the time, Pallas kernels for 0%

commit v1 on v0

v1 whole, which is shorter than its diff:
```python
import functools

import jax
import jax.numpy as jnp
from jax import lax
from jax.experimental import pallas as pl
from jax.experimental.pallas import tpu as pltpu
from jax.sharding import PartitionSpec as P

MESH = pl.DeviceIdType.MESH
AXIS = "shard"
BATCH = 4


def two_terms(x):
    high = x.astype(jnp.bfloat16)
    low = (x - high.astype(jnp.float32)).astype(jnp.bfloat16)
    return high, low


def kernel(
    groups,
    picked_ref,
    table_ref,
    dense_ref,
    small_ids_ref,
    scale_ids_ref,
    small_ref,
    out_ref,
    ids_buf,
    table_buf,
    small_buf,
    weights,
    counts,
    part_buf,
    recv_buf,
    local_sem,
    pair_send,
    pair_recv,
    ids_send,
    ids_recv,
    small_send,
    small_recv,
    part_send,
    part_recv,
):
    examples, picks = picked_ref.shape
    rows = table_ref.shape[0]
    small = small_ref.shape[0]
    batch = min(BATCH, groups)
    me = lax.axis_index(AXIS)
    core = lax.rem(me, 2)
    mine = lax.div(me, 2)
    partner = mine * 2 + 1 - core

    def peer(step):
        return lax.rem(mine + step + 1, groups)

    barrier = pltpu.get_barrier_semaphore()
    pl.semaphore_signal(barrier, inc=1, device_id=(partner,), device_id_type=MESH)

    def greet(step, _):
        pl.semaphore_signal(
            barrier, inc=1, device_id=(peer(step) * 2 + core,), device_id_type=MESH
        )
        return 0

    lax.fori_loop(0, groups - 1, greet, 0)

    own_rows = table_buf.at[pl.ds(pl.multiple_of(core * rows, rows), rows)]
    own_small = small_buf.at[pl.ds(pl.multiple_of(me * small, small), small)]
    table_in = pltpu.make_async_copy(table_ref, own_rows, local_sem.at[0])
    small_in = pltpu.make_async_copy(small_ref, own_small, local_sem.at[1])
    table_in.start()
    small_in.start()
    ids_buf[mine] = jnp.transpose(picked_ref[...])
    table_in.wait()
    small_in.wait()

    pl.semaphore_wait(barrier, groups)

    def ids_copy(slot, sem, to):
        return pltpu.make_async_remote_copy(
            src_ref=ids_buf.at[slot],
            dst_ref=ids_buf.at[slot],
            send_sem=ids_send.at[sem],
            recv_sem=ids_recv.at[slot],
            device_id=(to * 2 + core,),
            device_id_type=MESH,
        )

    def send_ids(step, _):
        ids_copy(mine, step, peer(step)).start()
        return 0

    lax.fori_loop(0, groups - 1, send_ids, 0)

    def pair_copy(src, dst, sem):
        return pltpu.make_async_remote_copy(
            src_ref=src,
            dst_ref=dst,
            send_sem=pair_send.at[sem],
            recv_sem=pair_recv.at[sem],
            device_id=(partner,),
            device_id_type=MESH,
        )

    pair_small = pair_copy(own_small, own_small, 0)
    pair_small.start()
    pair_table = pair_copy(own_rows, own_rows, 1)
    pair_table.start()
    pair_small.wait()

    def small_copy(slot, sem, to):
        block = small_buf.at[pl.ds(pl.multiple_of(slot * 2 * small, 2 * small), 2 * small)]
        return pltpu.make_async_remote_copy(
            src_ref=block,
            dst_ref=block,
            send_sem=small_send.at[sem],
            recv_sem=small_recv.at[slot],
            device_id=(to * 2 + core,),
            device_id_type=MESH,
        )

    def send_small(step, _):
        small_copy(mine, step, peer(step)).start()
        return 0

    lax.fori_loop(0, groups - 1, send_small, 0)

    pair_table.wait()
    high, low = two_terms(table_buf[...])
    features = high.shape[1]
    weights[:, :features] = high
    weights[:, features:] = low

    def part_copy(step, slot, to):
        return pltpu.make_async_remote_copy(
            src_ref=part_buf.at[pl.ds(pl.multiple_of(step * examples, examples), examples)],
            dst_ref=recv_buf.at[pl.ds(pl.multiple_of(slot * examples, examples), examples)],
            send_sem=part_send.at[step],
            recv_sem=part_recv.at[slot],
            device_id=(to * 2 + core,),
            device_id_type=MESH,
        )

    first = mine * (2 * rows)
    half = 16
    row_of = lax.broadcasted_iota(jnp.int32, (half, 2 * rows), 1)

    def serve(index, _):
        for q in range(batch):
            source = peer(index * batch + q)

            @pl.when(source != mine)
            def _():
                ids_copy(source, 0, source).wait_recv()

            wanted = jnp.transpose(ids_buf[source]) - first
            for h in range(examples // half):
                block = wanted[h * half : (h + 1) * half]
                count = jnp.zeros((half, 2 * rows), jnp.int32)
                for k in range(picks):
                    count = count + (block[:, k : k + 1] == row_of).astype(jnp.int32)
                counts[pl.ds(q * examples + h * half, half), :] = count.astype(
                    jnp.float32
                ).astype(jnp.bfloat16)
        both = jnp.dot(counts[...], weights[...], preferred_element_type=jnp.float32)
        total = both[:, :features] + both[:, features:]
        part_buf[
            pl.ds(pl.multiple_of(index * batch * examples, batch * examples), batch * examples), :
        ] = total
        for q in range(batch):
            step = index * batch + q
            to = peer(step)

            @pl.when(to != mine)
            def _():
                part_copy(step, mine, to).start()

        return 0

    lax.fori_loop(0, groups // batch, serve, 0)

    def take_small(step, _):
        source = peer(step)
        small_copy(source, 0, source).wait_recv()
        return 0

    lax.fori_loop(0, groups - 1, take_small, 0)

    all_small = small_buf.shape[0]
    small_row = lax.broadcasted_iota(jnp.int32, (all_small, examples), 0)
    table = small_buf[...]
    s_high, s_rest = table.astype(jnp.bfloat16), None
    rest = table - s_high.astype(jnp.float32)
    s_mid, s_low = two_terms(rest)

    def look_up(ids):
        chosen = jnp.where(ids == small_row, 1.0, 0.0).astype(jnp.bfloat16)

        def take(values):
            return lax.dot_general(
                chosen,
                values,
                (((0,), (0,)), ((), ())),
                preferred_element_type=jnp.float32,
            )

        return take(s_high) + take(s_mid) + take(s_low)

    small_rows = look_up(small_ids_ref[...])
    dense = dense_ref[...] * look_up(scale_ids_ref[...])

    def add(step, total):
        source = lax.rem(mine + groups - 1 - step, groups)
        part_copy(0, source, source).wait_recv()
        return total + recv_buf[
            pl.ds(pl.multiple_of(source * examples, examples), examples), :
        ]

    total = lax.fori_loop(0, groups - 1, add, part_buf[(groups - 1) * examples :, :])
    pooled = total * picks ** (-0.5)
    out_ref[0] = dense * pooled
    out_ref[1] = pooled * small_rows
    out_ref[2] = dense * small_rows

    def finish(step, _):
        ids_copy(mine, step, peer(step)).wait_send()
        small_copy(mine, step, peer(step)).wait_send()
        part_copy(step, mine, peer(step)).wait_send()
        return 0

    lax.fori_loop(0, groups - 1, finish, 0)


def local(picked_rows, main_table, dense_part, small_ids, small_table, scale_ids):
    devices = lax.axis_size(AXIS)
    groups = devices // 2
    examples, picks = picked_rows.shape
    rows, features = main_table.shape
    small = small_table.shape[0]
    vmem = pl.BlockSpec(memory_space=pltpu.VMEM)
    anywhere = pl.BlockSpec(memory_space=pl.ANY)
    dma = pltpu.SemaphoreType.DMA
    result = pl.pallas_call(
        functools.partial(kernel, groups),
        out_shape=jax.ShapeDtypeStruct((3, examples, features), jnp.float32),
        in_specs=[vmem, anywhere, vmem, vmem, vmem, anywhere],
        out_specs=vmem,
        scratch_shapes=[
            pltpu.VMEM((groups, picks, examples), jnp.int32),
            pltpu.VMEM((2 * rows, features), jnp.float32),
            pltpu.VMEM((devices * small, features), jnp.float32),
            pltpu.VMEM((2 * rows, 2 * features), jnp.bfloat16),
            pltpu.VMEM((min(BATCH, groups) * examples, 2 * rows), jnp.bfloat16),
            pltpu.VMEM((groups * examples, features), jnp.float32),
            pltpu.VMEM((groups * examples, features), jnp.float32),
            dma((2,)),
            dma((2,)),
            dma((2,)),
            dma((groups,)),
            dma((groups,)),
            dma((groups,)),
            dma((groups,)),
            dma((groups,)),
            dma((groups,)),
        ],
        compiler_params=pltpu.CompilerParams(collective_id=0, has_side_effects=True),
    )(
        picked_rows,
        main_table,
        dense_part,
        small_ids.reshape(1, examples),
        scale_ids.reshape(1, examples),
        small_table,
    )
    return jnp.transpose(result, (1, 0, 2))


def solution(mesh):
    placed = (
        P("shard", None),
        P("shard", None),
        P("shard", None),
        P("shard"),
        P("shard", None),
        P("shard"),
    )
    return jax.shard_map(
        local, mesh=mesh, in_specs=placed, out_specs=P("shard", None, None), check_vma=False
    )
```

time: 229 us -> 24.2 us (0.11)
  waiting for transfers between devices: 93.9 us -> 0 us
  blocking collectives: 80.8 us -> 0 us
  local copies, waits for them, and re-layouts: 30.1 us -> 2.79 us
  Pallas kernels: 0 us -> 21.1 us
  between operations: 13.5 us -> 0.01 us
  other arithmetic: 10.2 us -> 0 us
    reduce_scatter x1 -> x0, waiting for transfers between devices: 93.9 us -> none  [summed_rows(): return lax.psum_scatter(whole, axis, scatter_dimension=0, tiled=True)]
    all_gather x2 -> x0, blocking collectives: 80.8 us -> none  [the longest x1 44 us: local(): all_ids = lax.all_gather(picked_rows, 'shard', axis=0, tiled=True)]
    gather x3 -> x0, local copies, waits for them, and re-layouts: 29 us -> none  [the longest x1 27.8 us: rows_here(): jnp.take(table_part, jnp.clip(place, 0, table_part.shape[0] - 1), axis=0)]
    pallas_call x0 -> x1, Pallas kernels: none -> 21.1 us  [local(): pl.pallas_call(functools.partial(kernel, groups), out_shape=jax.ShapeDtyp...]
    reduce_sum x1 -> x0, other arithmetic: 8.69 us -> none  [pooled_part(): return jnp.sum(rows_here(main_table, wanted, big_first), axis=1)]
    unnamed x10 -> x2, local copies, waits for them, and re-layouts: 0.02 us -> 2.79 us
  transfers between devices with their start and end apart: 1 -> 0, of which waited for: 1 -> 0; matrix products, arithmetic and copies ran while one was open for 1% -> 0% of each run, Pallas kernels for 0% -> 0%
where the time goes in v1:
time: 24.2 us; the launch traced here: 23.9 us
  Pallas kernels  21.1 us (87%)
  local copies, waits for them, and re-layouts  2.79 us (12%)
    pallas_call x1, Pallas kernels, local(): pl.pallas_call(functools.partial(kernel, groups), out_shape=jax.ShapeDtyp...  21.1 us
    unnamed x2, local copies, waits for them, and re-layouts  2.79 us

profile of v1, /device:TPU:0, one launch (start us, length us, event | category | flops | bytes accessed | tf_op | source)
XLA Modules:
  0.0 23.9 jit_solution(6590589962289094604)
XLA Ops:
  0.0 1.4 %copy.7.picked_ref = s32[32,8]{1,0:T(8,128)} copy(s32[32,8]{0,1:T(8,128)} %param.6) | data formatting | bytes 2048 | tf_op args[0]
  1.4 21.1 %shard_map.64 = f32[3,32,128]{2,1,0:T(8,128)} custom-call(s32[32,8]{1,0:T(8,128)} %copy.7.picked_ref, f32[512,128]{1,0:T(8,128)} %table_ref.1, f32[32,128]{1,0:T(8,128)} %dense_ref.1, s32[1,32]{1,0:T(1,128)} %bitcast.4, s32[1,32]{1,0:T(1,128)} %bitcast.5, f32[4,128]{1,0:T(4,128)} %small_ref.1), custom_call_target="tpu_custom_call" | custom-call | tf_op jit(solution)/shard_map/pallas_call | solution.py:246
  22.5 1.4 %copy.9 = f32[32,3,128]{2,0,1:T(8,128)} copy(f32[32,3,128]{2,0,1:T(8,128)} %bitcast.3) | data formatting | bytes 98304

commit v2 on v1

--- a/solution.py
+++ b/solution.py
@@ -30,6 +30,8 @@
     ids_buf,
     table_buf,
     small_buf,
+    dense_buf,
+    lookup_buf,
     weights,
     counts,
     part_buf,
@@ -44,7 +46,7 @@
     part_send,
     part_recv,
 ):
-    examples, picks = picked_ref.shape
+    picks, examples = picked_ref.shape
     rows = table_ref.shape[0]
     small = small_ref.shape[0]
     batch = min(BATCH, groups)
@@ -69,14 +71,20 @@
 
     own_rows = table_buf.at[pl.ds(pl.multiple_of(core * rows, rows), rows)]
     own_small = small_buf.at[pl.ds(pl.multiple_of(me * small, small), small)]
+    ids_in = pltpu.make_async_copy(picked_ref, ids_buf.at[mine], local_sem.at[2])
+    ids_in.start()
     table_in = pltpu.make_async_copy(table_ref, own_rows, local_sem.at[0])
     small_in = pltpu.make_async_copy(small_ref, own_small, local_sem.at[1])
     table_in.start()
     small_in.start()
-    ids_buf[mine] = jnp.transpose(picked_ref[...])
-    table_in.wait()
+    dense_in = pltpu.make_async_copy(dense_ref, dense_buf, local_sem.at[3])
+    first_in = pltpu.make_async_copy(small_ids_ref, lookup_buf.at[0], local_sem.at[4])
+    second_in = pltpu.make_async_copy(scale_ids_ref, lookup_buf.at[1], local_sem.at[5])
+    dense_in.start()
+    first_in.start()
+    second_in.start()
+    ids_in.wait()
     small_in.wait()
-
     pl.semaphore_wait(barrier, groups)
 
     def ids_copy(slot, sem, to):
@@ -107,6 +115,7 @@
 
     pair_small = pair_copy(own_small, own_small, 0)
     pair_small.start()
+    table_in.wait()
     pair_table = pair_copy(own_rows, own_rows, 1)
     pair_table.start()
     pair_small.wait()
@@ -209,8 +218,11 @@
 
         return take(s_high) + take(s_mid) + take(s_low)
 
-    small_rows = look_up(small_ids_ref[...])
-    dense = dense_ref[...] * look_up(scale_ids_ref[...])
+    dense_in.wait()
+    first_in.wait()
+    second_in.wait()
+    small_rows = look_up(lookup_buf[0])
+    dense = dense_buf[...] * look_up(lookup_buf[1])
 
     def add(step, total):
         source = lax.rem(mine + groups - 1 - step, groups)
@@ -246,17 +258,19 @@
     result = pl.pallas_call(
         functools.partial(kernel, groups),
         out_shape=jax.ShapeDtypeStruct((3, examples, features), jnp.float32),
-        in_specs=[vmem, anywhere, vmem, vmem, vmem, anywhere],
+        in_specs=[anywhere] * 6,
         out_specs=vmem,
         scratch_shapes=[
             pltpu.VMEM((groups, picks, examples), jnp.int32),
             pltpu.VMEM((2 * rows, features), jnp.float32),
             pltpu.VMEM((devices * small, features), jnp.float32),
+            pltpu.VMEM((examples, features), jnp.float32),
+            pltpu.VMEM((2, 1, examples), jnp.int32),
             pltpu.VMEM((2 * rows, 2 * features), jnp.bfloat16),
             pltpu.VMEM((min(BATCH, groups) * examples, 2 * rows), jnp.bfloat16),
             pltpu.VMEM((groups * examples, features), jnp.float32),
             pltpu.VMEM((groups * examples, features), jnp.float32),
-            dma((2,)),
+            dma((6,)),
             dma((2,)),
             dma((2,)),
             dma((groups,)),
@@ -268,7 +282,7 @@
         ],
         compiler_params=pltpu.CompilerParams(collective_id=0, has_side_effects=True),
     )(
-        picked_rows,
+        jnp.transpose(picked_rows),
         main_table,
         dense_part,
         small_ids.reshape(1, examples),

time: 24.2 us -> 22 us (0.909)
  local copies, waits for them, and re-layouts: 2.79 us -> 1.42 us
  Pallas kernels: 21.1 us -> 20.4 us
    unnamed x2 -> x1, local copies, waits for them, and re-layouts: 2.79 us -> 1.42 us
    pallas_call x1, Pallas kernels: 21.1 us -> 20.4 us  [local(): pl.pallas_call(functools.partial(kernel, groups), out_shape=jax.ShapeDtyp...]
where the time goes in v2:
time: 22 us; the launch traced here: 21.8 us
  Pallas kernels  20.4 us (93%)
  local copies, waits for them, and re-layouts  1.42 us (6%)
    pallas_call x1, Pallas kernels, local(): pl.pallas_call(functools.partial(kernel, groups), out_shape=jax.ShapeDtyp...  20.4 us
    unnamed x1, local copies, waits for them, and re-layouts  1.42 us

profile of v2, /device:TPU:0, one launch (start us, length us, event | category | flops | bytes accessed | tf_op | source)
XLA Modules:
  0.0 21.8 jit_solution(4728364334164781850)
XLA Ops:
  0.0 20.4 %shard_map.64 = f32[3,32,128]{2,1,0:T(8,128)} custom-call(s32[8,32]{1,0:T(8,128)} %bitcast.5, f32[512,128]{1,0:T(8,128)} %table_ref.1, f32[32,128]{1,0:T(8,128)} %dense_ref.1, s32[1,32]{1,0:T(1,128)} %bitcast.6, s32[1,32]{1,0:T(1,128)} %bitcast.7, f32[4,128]{1,0:T(4,128)} %small_ref.1), custom_call_target="tpu_custom_call" | custom-call | tf_op jit(solution)/shard_map/pallas_call | solution.py:258
  20.4 1.4 %copy.8 = f32[32,3,128]{2,0,1:T(8,128)} copy(f32[32,3,128]{2,0,1:T(8,128)} %bitcast.4) | data formatting | bytes 98304

commit v3 on v2

--- a/solution.py
+++ b/solution.py
@@ -257,7 +257,7 @@
     dma = pltpu.SemaphoreType.DMA
     result = pl.pallas_call(
         functools.partial(kernel, groups),
-        out_shape=jax.ShapeDtypeStruct((3, examples, features), jnp.float32),
+        out_shape=pltpu.VMEM((3, examples, features), jnp.float32),
         in_specs=[anywhere] * 6,
         out_specs=vmem,
         scratch_shapes=[

time: 22 us -> 20.6 us (0.936)
  local copies, waits for them, and re-layouts: 1.42 us -> 0.62 us
  Pallas kernels: 20.4 us -> 19.8 us
    unnamed x1, local copies, waits for them, and re-layouts: 1.42 us -> 0.62 us
    pallas_call x1, Pallas kernels: 20.4 us -> 19.8 us  [local(): pl.pallas_call(functools.partial(kernel, groups), out_shape=pltpu.VMEM((3...]
where the time goes in v3:
time: 20.6 us; the launch traced here: 20.4 us
  Pallas kernels  19.8 us (96%)
  local copies, waits for them, and re-layouts  0.62 us (3%)
    pallas_call x1, Pallas kernels, local(): pl.pallas_call(functools.partial(kernel, groups), out_shape=pltpu.VMEM((3...  19.8 us
    unnamed x1, local copies, waits for them, and re-layouts  0.62 us

profile of v3, /device:TPU:0, one launch (start us, length us, event | category | flops | bytes accessed | tf_op | source)
XLA Modules:
  0.0 20.4 jit_solution(8030235775093295973)
XLA Ops:
  0.0 19.8 %shard_map.64 = f32[3,32,128]{2,1,0:T(8,128)S(1)} custom-call(s32[8,32]{1,0:T(8,128)} %bitcast.5, f32[512,128]{1,0:T(8,128)} %table_ref.1, f32[32,128]{1,0:T(8,128)} %dense_ref.1, s32[1,32]{1,0:T(1,128)} %bitcast.6, s32[1,32]{1,0:T(1,128)} %bitcast.7, f32[4,128]{1,0:T(4,128)} %small_ref.1), custom_call_target="tpu_custom_call" | custom-call | tf_op jit(solution)/shard_map/pallas_call | solution.py:258
  19.8 0.6 %copy.8 = f32[32,3,128]{2,0,1:T(8,128)} copy(f32[32,3,128]{2,0,1:T(8,128)S(1)} %bitcast.4) | data formatting | bytes 98304

commit v4 on v3

--- a/solution.py
+++ b/solution.py
@@ -55,13 +55,23 @@
     mine = lax.div(me, 2)
     partner = mine * 2 + 1 - core
 
+    within = lax.rem(mine, batch)
+    base = mine - within
+
     def peer(step):
-        return lax.rem(mine + step + 1, groups)
+        block = lax.div(step, batch)
+        side = 1 - 2 * lax.rem(block + 1, 2)
+        start = jnp.where(block == 0, 0, groups // 2 + side * batch * lax.div(block, 2))
+        return lax.rem(base + start, groups) + lax.rem(within + step, batch)
+
+    def far_first(index):
+        return 1 + lax.rem(index + batch - 1, groups - 1)
 
     barrier = pltpu.get_barrier_semaphore()
     pl.semaphore_signal(barrier, inc=1, device_id=(partner,), device_id_type=MESH)
 
-    def greet(step, _):
+    def greet(index, _):
+        step = far_first(index)
         pl.semaphore_signal(
             barrier, inc=1, device_id=(peer(step) * 2 + core,), device_id_type=MESH
         )
@@ -97,7 +107,8 @@
             device_id_type=MESH,
         )
 
-    def send_ids(step, _):
+    def send_ids(index, _):
+        step = far_first(index)
         ids_copy(mine, step, peer(step)).start()
         return 0
 
@@ -135,7 +146,7 @@
         small_copy(mine, step, peer(step)).start()
         return 0
 
-    lax.fori_loop(0, groups - 1, send_small, 0)
+    lax.fori_loop(1, groups, send_small, 0)
 
     pair_table.wait()
     high, low = two_terms(table_buf[...])
@@ -196,7 +207,7 @@
         small_copy(source, 0, source).wait_recv()
         return 0
 
-    lax.fori_loop(0, groups - 1, take_small, 0)
+    lax.fori_loop(1, groups, take_small, 0)
 
     all_small = small_buf.shape[0]
     small_row = lax.broadcasted_iota(jnp.int32, (all_small, examples), 0)
@@ -225,13 +236,13 @@
     dense = dense_buf[...] * look_up(lookup_buf[1])
 
     def add(step, total):
-        source = lax.rem(mine + groups - 1 - step, groups)
+        source = peer(step)
         part_copy(0, source, source).wait_recv()
         return total + recv_buf[
             pl.ds(pl.multiple_of(source * examples, examples), examples), :
         ]
 
-    total = lax.fori_loop(0, groups - 1, add, part_buf[(groups - 1) * examples :, :])
+    total = lax.fori_loop(1, groups, add, part_buf[:examples, :])
     pooled = total * picks ** (-0.5)
     out_ref[0] = dense * pooled
     out_ref[1] = pooled * small_rows
@@ -243,7 +254,7 @@
         part_copy(step, mine, peer(step)).wait_send()
         return 0
 
-    lax.fori_loop(0, groups - 1, finish, 0)
+    lax.fori_loop(1, groups, finish, 0)
 
 
 def local(picked_rows, main_table, dense_part, small_ids, small_table, scale_ids):

time: 20.6 us -> 20.7 us (level)
  no operation moved by 1% of the time
where the time goes in v4:
time: 20.7 us; the launch traced here: 20.5 us
  Pallas kernels  19.9 us (96%)
  local copies, waits for them, and re-layouts  0.62 us (3%)
    pallas_call x1, Pallas kernels, local(): pl.pallas_call(functools.partial(kernel, groups), out_shape=pltpu.VMEM((3...  19.9 us
    unnamed x1, local copies, waits for them, and re-layouts  0.62 us

profile of v4, /device:TPU:0, one launch (start us, length us, event | category | flops | bytes accessed | tf_op | source)
XLA Modules:
  0.0 20.5 jit_solution(6400894280178359206)
XLA Ops:
  0.0 19.9 %shard_map.64 = f32[3,32,128]{2,1,0:T(8,128)S(1)} custom-call(s32[8,32]{1,0:T(8,128)} %bitcast.5, f32[512,128]{1,0:T(8,128)} %table_ref.1, f32[32,128]{1,0:T(8,128)} %dense_ref.1, s32[1,32]{1,0:T(1,128)} %bitcast.6, s32[1,32]{1,0:T(1,128)} %bitcast.7, f32[4,128]{1,0:T(4,128)} %small_ref.1), custom_call_target="tpu_custom_call" | custom-call | tf_op jit(solution)/shard_map/pallas_call | solution.py:269
  19.9 0.6 %copy.8 = f32[32,3,128]{2,0,1:T(8,128)} copy(f32[32,3,128]{2,0,1:T(8,128)S(1)} %bitcast.4) | data formatting | bytes 98304
